TPU v7x, 32 devices: a whole 2x2x4 slice. The times are simulated.
32 devices in a mesh: ent: 16 (over z, y, x), dim: 2 (over core).
Axes of the slice: x: 2, y: 2, z: 4, core: 2. Of those that a mesh axis runs over, the one named last changes fastest.
Arguments:
- entities: float32 [32768, 1024], P('ent', 'dim'), may hold values from -3 to 3
- ent_state: float32 [32768], P('ent'), may hold values from 0.01 to 0.1
- buckets: int32 [32768], P('ent'), may hold values from 0 to 7
- relations: float32 [4096, 1024], P(None, 'dim'), may hold values from -1.6 to 1.6
- rel_state: float32 [4096], replicated, may hold values from 0.05 to 0.5
- triples: int32 [3, 8192], P(None, 'ent'), may hold values from 0 to 32767, as said below
- negatives: int32 [32, 256], P('ent'), may hold values from 0 to 32767, as said below
Outputs:
- new_entities: float32 [32768, 1024], P('ent', 'dim')
- new_relations: float32 [4096, 1024], P(None, 'dim')
Inputs may be any that keep to these rules, and one draw needn't show every extreme that they name: `triples`: rows 0 and 2 hold entity ids, row 1 relation ids below 4096. The block of an entity id is id // 2048. Among the 768 ids of one group (its heads, its tails and its negatives) at most 128 lie in one block, and in every draw, for each rank of a group among the 2 groups of an index of ent, some block holds exactly 128 ids of that group on every index of ent. `negatives`: entity ids; they count in the bound on the ids of a group stated for triples.
All inputs are finite; a program needn't handle non-finite values.
Results may differ from a plain program's by a relative error of at most 0.0017.
Values may be sent and summed in bfloat16 or wider, within the bound.
A program may use at most 128 MiB of HBM per device.

v0:
```python
import jax
import jax.numpy as jnp
from jax import lax
from jax.sharding import PartitionSpec as P

RANK = 512
BLK = 64


LEARN_RATE = 0.1
REG_WEIGHT = 0.01


def halves(values):
    shaped = values.reshape(values.shape[:-1] + (values.shape[-1] // (2 * BLK), 2, BLK))
    return (shaped[..., 0, :], shaped[..., 1, :])


def joined(real_part, imag_part):
    stacked = jnp.stack([real_part, imag_part], axis=-2)
    return stacked.reshape(stacked.shape[:-3] + (stacked.shape[-3] * 2 * BLK,))


def complex_product(former, latter):
    former_re, former_im = halves(former)
    latter_re, latter_im = halves(latter)
    return joined(
        former_re * latter_re - former_im * latter_im, former_re * latter_im + former_im * latter_re
    )


def conjugate(values):
    real_part, imag_part = halves(values)
    return joined(real_part, -imag_part)


def rounded(values):
    return lax.optimization_barrier(values.astype(jnp.bfloat16))


def contract_first(former, latter):
    return lax.dot_general(
        former, latter, (((0,), (0,)), ((), ())), preferred_element_type=jnp.float32
    )


def contract_last(former, latter):
    return lax.dot_general(
        former, latter, (((1,), (1,)), ((), ())), preferred_element_type=jnp.float32
    )


def coefficients(pos_score, both_score, width_neg):
    return (rounded(-jax.nn.sigmoid(-pos_score)), rounded(jax.nn.sigmoid(both_score) / width_neg))


def group_step(rows_group, rel_group, rel_low, group_len):
    head_float = rows_group[:group_len].astype(jnp.float32)
    tail_float = rows_group[group_len : 2 * group_len].astype(jnp.float32)
    noise_rows = rows_group[2 * group_len :]
    width_neg = noise_rows.shape[0]
    rel_float = jnp.take(rel_low, rel_group, axis=0).astype(jnp.float32)
    query = rounded(complex_product(head_float, rel_float))
    probe = rounded(complex_product(conjugate(rel_float), tail_float))
    part_pos = jnp.sum(query.astype(jnp.float32) * tail_float, axis=-1)
    part_both = jnp.stack(
        [contract_last(query, noise_rows), contract_last(probe, noise_rows)], axis=1
    )
    pos_share, both_share = (
        lax.psum_scatter(
            part_pos.astype(jnp.bfloat16), "dim", scatter_dimension=0, tiled=True
        ).astype(jnp.float32),
        lax.psum_scatter(
            part_both.astype(jnp.bfloat16), "dim", scatter_dimension=0, tiled=True
        ).astype(jnp.float32),
    )
    pos_part, both_part = coefficients(pos_share, both_share, width_neg)
    pos_coef, both_coef = (
        lax.all_gather(pos_part, "dim", axis=0, tiled=True),
        lax.all_gather(both_part, "dim", axis=0, tiled=True),
    )
    tail_coef = both_coef[:, 0]
    head_coef = both_coef[:, 1]
    pos_float = pos_coef.astype(jnp.float32)
    tail_pull = pos_float[:, None] * tail_float + jnp.dot(
        tail_coef, noise_rows, preferred_element_type=jnp.float32
    )
    head_pull = jnp.dot(head_coef, noise_rows, preferred_element_type=jnp.float32)
    head_side = pos_float[:, None] * head_float + head_pull
    head_grad = complex_product(conjugate(rel_float), tail_pull).astype(jnp.bfloat16)
    tail_grad = complex_product(rel_float, head_side).astype(jnp.bfloat16)
    noise_grad = (contract_first(tail_coef, query) + contract_first(head_coef, probe)).astype(
        jnp.bfloat16
    )
    rel_grad = complex_product(conjugate(head_float), tail_pull) + complex_product(
        tail_float, conjugate(head_pull)
    )
    rel_hits = (
        rel_group[:, None] == jnp.arange(rel_low.shape[0], dtype=jnp.int32)[None, :]
    ).astype(jnp.float32)
    rel_part = lax.dot_general(
        rel_hits,
        rel_grad,
        (((0,), (0,)), ((), ())),
        precision=lax.Precision.HIGHEST,
        preferred_element_type=jnp.float32,
    )
    return (jnp.concatenate([head_grad, tail_grad, noise_grad], axis=0), rel_part)


def look_up(received, ent_low, row_base):
    local_rows = received - row_base
    picked = jnp.take(ent_low, jnp.clip(local_rows, 0, ent_low.shape[0] - 1), axis=0)
    return jnp.where((received >= 0)[..., None], picked, jnp.zeros((), jnp.bfloat16))


def placement_of(wanted_row, owners, rows_here, slot_count):
    request_count = wanted_row.shape[0]
    owner_of = wanted_row // rows_here
    owner_hits = (owner_of[:, None] == jnp.arange(owners, dtype=jnp.int32)[None, :]).astype(
        jnp.bfloat16
    )
    order = jnp.arange(request_count, dtype=jnp.int32)
    earlier = (order[:, None] > order[None, :]).astype(jnp.bfloat16)
    before = jnp.dot(earlier, owner_hits, preferred_element_type=jnp.float32)
    slot_rank = jnp.sum(before * owner_hits.astype(jnp.float32), axis=-1).astype(jnp.int32)
    slot_flat = owner_of * slot_count + slot_rank
    matches = slot_flat[:, None] == jnp.arange(owners * slot_count, dtype=jnp.int32)[None, :]
    slot_ids = jnp.sum(jnp.where(matches, wanted_row[:, None], 0), axis=0)
    slot_ids = jnp.where(jnp.any(matches, axis=0), slot_ids, -1)
    return (matches.astype(jnp.bfloat16), slot_ids.reshape(owners, slot_count))


def accumulate(received_ids, received_rows, row_base, totals, counts):
    flat_ids = received_ids.reshape(-1)
    flat_rows = received_rows.reshape(flat_ids.shape[0], received_rows.shape[-1])
    slot_total = flat_ids.shape[0]
    block_size = 1024
    positions = jnp.arange(totals.shape[0], dtype=jnp.int32)
    for first_slot in range(0, slot_total, block_size):
        local_rows = flat_ids[first_slot : first_slot + block_size] - row_base
        one_hot = (local_rows[:, None] == positions[None, :]).astype(jnp.bfloat16)
        totals = totals + contract_first(one_hot, flat_rows[first_slot : first_slot + block_size])
        counts = counts + jnp.sum(one_hot, axis=0, dtype=jnp.float32)
    return (totals, counts)


def adagrad(table, state, grad, squares):
    new_state = state + squares / (2 * RANK)
    return table - LEARN_RATE * grad / jnp.sqrt(new_state)[:, None]


def per_device(entities, ent_state, buckets, relations, rel_state, triples, negatives):
    owners = lax.axis_size("ent")
    rows_here = entities.shape[0]
    columns_here = entities.shape[1]
    row_base = lax.axis_index("ent") * rows_here
    groups_here = negatives.shape[0]
    group_len = triples.shape[1] // groups_here
    request_count = 2 * group_len + negatives.shape[1]
    slot_count = 8 * ((request_count + 3 * owners - 1) // (3 * owners))
    ent_low = entities.astype(jnp.bfloat16)
    rel_low = relations.astype(jnp.bfloat16)
    head_ids = triples[0].reshape(groups_here, group_len)
    rel_ids = triples[1].reshape(groups_here, group_len)
    tail_ids = triples[2].reshape(groups_here, group_len)
    wanted = jnp.concatenate([head_ids, tail_ids, negatives], axis=1)
    placed = [
        placement_of(wanted[index], owners, rows_here, slot_count) for index in range(groups_here)
    ]
    totals = jnp.zeros((rows_here, columns_here), jnp.float32)
    counts = jnp.zeros((rows_here,), jnp.float32)
    rel_total = jnp.zeros((relations.shape[0], columns_here), jnp.float32)
    for index in range(groups_here):
        matches, slot_ids = placed[index]
        received = lax.all_to_all(slot_ids, "ent", split_axis=0, concat_axis=0, tiled=True)
        arrived = lax.all_to_all(
            look_up(received, ent_low, row_base), "ent", split_axis=0, concat_axis=0, tiled=True
        )
        rows_group = jnp.dot(
            matches,
            arrived.reshape(owners * slot_count, columns_here),
            preferred_element_type=jnp.float32,
        ).astype(jnp.bfloat16)
        grads, rel_part = group_step(rows_group, rel_ids[index], rel_low, group_len)
        outgoing = (
            contract_first(matches, grads)
            .astype(jnp.bfloat16)
            .reshape(owners, slot_count, columns_here)
        )
        returned = lax.all_to_all(outgoing, "ent", split_axis=0, concat_axis=0, tiled=True)
        totals, counts = accumulate(received, returned, row_base, totals, counts)
        rel_total = rel_total + rel_part
    weight = REG_WEIGHT * (buckets.astype(jnp.float32) + 1.0) * counts
    totals = totals + weight[:, None] * 3.0 * entities * jnp.abs(entities)
    ent_squares = jnp.sum(totals * totals, axis=-1)
    rel_grad = lax.psum(rel_total, "ent")
    ent_all, rel_all = lax.psum((ent_squares, jnp.sum(rel_grad * rel_grad, axis=-1)), "dim")
    new_relations = adagrad(relations, rel_state, rel_grad, rel_all)
    new_entities = adagrad(entities, ent_state, totals, ent_all)
    return (new_entities, new_relations)


def solution(mesh):
    placed = (
        P("ent", "dim"),
        P("ent"),
        P("ent"),
        P(None, "dim"),
        P(),
        P(None, "ent"),
        P("ent", None),
    )
    return jax.shard_map(
        per_device,
        mesh=mesh,
        in_specs=placed,
        out_specs=(P("ent", "dim"), P(None, "dim")),
        check_vma=False,
    )
```

profile of v0, /device:TPU:0, one launch (start us, length us, event | category | flops | bytes accessed | tf_op | source)
XLA Modules:
  0.0 564.8 jit_solution(14745448895838830831)
XLA Ops:
  9.5 1.1 fusion.10
  10.6 1.9 select_reduce_fusion
  13.1 8.3 %all-to-all-start.3 = ((s32[16,1,128]{2,1,0:T(1,128)}), s32[16,1,128]{2,1,0:T(1,128)S(1)}, u32[]{:S(2)}, u32[]{:S(2)}) async-start(s32[16,1,128]{2,1,0:T(1,128)} %bitcast.29), calls=%async_computation.4 | async-start | bytes 16384 | tf_op jit(solution)/shard_map/all_to_all | solution.py:176
  21.5 1.1 fusion.13
  23.2 2.5 convert_element_type.177
  25.6 3.1 all-to-all-done.3
  28.7 3.9 all-to-all-start
  32.6 9.2 %gather_fusion.3 = bf16[2048,512]{1,0:T(8,128)(2,1)} fusion(bf16[2048,512]{1,0:T(8,128)(2,1)S(1)} %convert_element_type.177, s32[2048]{0:T(1024)S(1)} %bitcast_clamp_fusion), kind=kCustom, calls=%fused_computation.3.clone | custom fusion | bytes 4202496 | tf_op jit(solution)/shard_map/jit(_take)/gather | solution.py:113
  41.8 2.9 select_select_fusion
  44.7 7.0 %all-to-all-start.4 = ((bf16[16,128,512]{2,1,0:T(8,128)(2,1)}), bf16[16,128,512]{2,1,0:T(8,128)(2,1)}, u32[]{:S(2)}, u32[]{:S(2)}) async-start(bf16[16,128,512]{2,1,0:T(8,128)(2,1)} %select_select_fusion), calls=%async_computation.5 | async-start | bytes 4194304 | tf_op jit(solution)/shard_map/all_to_all | solution.py:177
  51.7 9.2 %gather_fusion.1 = bf16[2048,512]{1,0:T(8,128)(2,1)} fusion(bf16[2048,512]{1,0:T(8,128)(2,1)S(1)} %convert_element_type.177, s32[2048]{0:T(1024)S(1)} %bitcast_clamp_fusion.1), kind=kCustom, calls=%fused_computation.1.clone | custom fusion | bytes 4202496 | tf_op jit(solution)/shard_map/jit(_take)/gather | solution.py:113
  60.9 2.9 select_select_fusion.1
  63.8 30.1 %all-to-all-done.4 = bf16[16,128,512]{2,1,0:T(8,128)(2,1)} async-done(((bf16[16,128,512]{2,1,0:T(8,128)(2,1)}), bf16[16,128,512]{2,1,0:T(8,128)(2,1)}, u32[]{:S(2)}, u32[]{:S(2)}) %all-to-all-start.4) | async-done | bytes 2097184 | tf_op jit(solution)/shard_map/all_to_all | solution.py:177
  93.9 9.9 %all-to-all-start.1 = ((bf16[16,128,512]{2,1,0:T(8,128)(2,1)}), bf16[16,128,512]{2,1,0:T(8,128)(2,1)}, u32[]{:S(2)}, u32[]{:S(2)}) async-start(bf16[16,128,512]{2,1,0:T(8,128)(2,1)} %select_select_fusion.1), calls=%async_computation.1 | async-start | bytes 4194304 | tf_op jit(solution)/shard_map/all_to_all | solution.py:177
  104.0 5.9 %convert_element_type.176 = bf16[4096,512]{1,0:T(8,128)(2,1)} convert(f32[4096,512]{1,0:T(8,128)} %param.14) | non-fusion elementwise | flops 2097152 | bytes 12582912 | tf_op jit(solution)/shard_map/convert_element_type | solution.py:163
  110.7 3.9 gather_fusion.2
  114.7 3.9 gather_fusion
  120.6 3.7 fusion.34
  125.5 20.9 %all-to-all-done.1 = bf16[16,128,512]{2,1,0:T(8,128)(2,1)} async-done(((bf16[16,128,512]{2,1,0:T(8,128)(2,1)}), bf16[16,128,512]{2,1,0:T(8,128)(2,1)}, u32[]{:S(2)}, u32[]{:S(2)}) %all-to-all-start.1) | async-done | bytes 2097184 | tf_op jit(solution)/shard_map/all_to_all | solution.py:177
  146.4 3.7 fusion.33
  151.9 1.2 fusion.40
  154.2 1.1 multiply_reduce_fusion.3
  156.0 2.6 all-reduce.3
  158.7 1.8 all-gather.1
  161.1 1.8 all-gather
  163.5 1.2 fusion.37
  164.7 1.3 fusion.38
  167.8 2.0 all_gather.15
  169.8 1.3 convolution_add_fusion.2
  171.1 1.2 fusion.66
  172.4 1.9 fusion.36
  174.3 2.1 multiply_add_fusion.1
  176.4 2.5 reduce-scatter.3.cloned.1.call-done
  179.8 2.1 all_gather.13
  183.4 4.3 fusion.25
  187.7 7.5 %all-to-all-start.5 = ((bf16[16,128,512]{2,1,0:T(8,128)(2,1)}), bf16[16,128,512]{2,1,0:T(8,128)(2,1)S(1)}, u32[]{:S(2)}, u32[]{:S(2)}) async-start(bf16[16,128,512]{2,1,0:T(8,128)(2,1)} %bitcast.139), calls=%async_computation.7 | async-start | bytes 4194304 | tf_op jit(solution)/shard_map/all_to_all | solution.py:191
  195.6 2.3 multiply_add_fusion.2
  198.0 1.4 convolution_add_fusion.4
  199.4 1.1 multiply_subtract_fusion.2
  201.6 4.9 fusion.29
  206.5 7.3 %convolution_add_fusion = f32[4096,512]{1,0:T(8,128)} fusion(f32[4096,512]{1,0:T(8,128)S(1)} %fusion.29, f32[256,512]{0,1:T(8,128)S(1)} %bitcast.135, s32[256]{0:T(256)S(1)} %bitcast.165), kind=kOutput, calls=%fused_computation.22 | convolution fusion | flops 6446645248 | bytes 17302528 | tf_op jit(solution)/shard_map/dot_general | solution.py:101
  213.9 1.2 subtract_convert_fusion.4
  218.0 1.2 fusion.35
  219.3 4.4 fusion.24
  223.7 33.7 %all-to-all-done.5 = bf16[16,128,512]{2,1,0:T(8,128)(2,1)S(1)} async-done(((bf16[16,128,512]{2,1,0:T(8,128)(2,1)}), bf16[16,128,512]{2,1,0:T(8,128)(2,1)S(1)}, u32[]{:S(2)}, u32[]{:S(2)}) %all-to-all-start.5) | async-done | bytes 2097184 | tf_op jit(solution)/shard_map/all_to_all | solution.py:191
  257.4 27.7 %all-to-all-start.2 = ((bf16[16,128,512]{2,1,0:T(8,128)(2,1)}), bf16[16,128,512]{2,1,0:T(8,128)(2,1)}, u32[]{:S(2)}, u32[]{:S(2)}) async-start(bf16[16,128,512]{2,1,0:T(8,128)(2,1)} %bitcast.140), calls=%async_computation.3 | async-start | bytes 4194304 | tf_op jit(solution)/shard_map/all_to_all | solution.py:191
  285.1 5.5 copy.89
  290.6 1.0 convert_reduce_fusion.3
  291.7 1.0 convert_reduce_fusion.2
  292.7 1.0 convert_reduce_fusion.1
  293.8 1.0 convert_reduce_fusion
  294.9 1.2 fusion.81
  296.1 54.5 %all-to-all-done.2 = bf16[16,128,512]{2,1,0:T(8,128)(2,1)} async-done(((bf16[16,128,512]{2,1,0:T(8,128)(2,1)}), bf16[16,128,512]{2,1,0:T(8,128)(2,1)}, u32[]{:S(2)}, u32[]{:S(2)}) %all-to-all-start.2) | async-done | bytes 2097184 | tf_op jit(solution)/shard_map/all_to_all | solution.py:191
  350.5 1.7 fusion.82
  352.3 2.7 fusion.7
  355.0 2.7 fusion.5
  357.8 3.0 fusion.3
  360.8 5.7 %multiply_reduce_fusion.1 = (f32[2048]{0:T(1024)S(1)}, f32[2048,512]{0,1:T(8,128)}) fusion(f32[2048,512]{0,1:T(8,128)S(1)} %copy-done, f32[2048]{0:T(1024)S(1)} %multiply_multiply_fusion, bf16[1024,512]{1,0:T(8,128)(2,1)S(1)} %bitcast.153, s32[1024]{0:T(1024)S(1)} %bitcast.174, f32[2048,512]{0,1:T(8,128)S(1)} %fusion.3, f32[2048,512]{0,1:T(8,128)S(1)} %fusion.7, ...), kind=kOutput, calls=%fused_computation.36 | convolution fusion | flops 2159015936 | bytes 22040576 | tf_op jit(solution)/shard_map/dot_general | solution.py:42
  366.5 161.9 %all-reduce.6.cloned.1.call-done = f32[4096,512]{1,0:T(8,128)} async-done(((f32[4096,512]{1,0:T(8,128)}), f32[4096,512]{1,0:T(8,128)}) %all-reduce.6.cloned.1.call-update) | async-done | bytes 8388624 | tf_op jit(solution)/shard_map/psum | solution.py:197
  528.4 4.0 multiply_reduce_fusion
  532.4 3.4 all-reduce.2
  535.8 6.8 %divide_subtract_fusion.1 = f32[2048,512]{0,1:T(8,128)} fusion(f32[2048,512]{0,1:T(8,128)} %copy.89, f32[2048,512]{0,1:T(8,128)} %get-tuple-element.73, f32[2048]{0:T(1024)S(1)} %add_sqrt_fusion.1), kind=kLoop, calls=%fused_computation.35 | loop fusion | flops 3145728 | bytes 12591104 | tf_op jit(solution)/shard_map/sub | solution.py:150
  542.7 5.3 copy.92
  548.0 10.0 %divide_subtract_fusion = f32[4096,512]{1,0:T(8,128)} fusion(f32[4096,512]{1,0:T(8,128)} %param.14, f32[4096,512]{1,0:T(8,128)} %all-reduce.6.cloned.1.call-done, f32[4096]{0:T(1024)S(1)} %add_sqrt_fusion), kind=kLoop, calls=%fused_computation.4 | loop fusion | flops 6291456 | bytes 25182208 | tf_op jit(solution)/shard_map/sub | solution.py:150
  (128 shorter events, 20.5 us)
Async XLA Ops:
  9.1 14.1 %copy-start.21 = (s32[768]{0:T(1024)}, s32[768]{0:T(1024)S(1)}, u32[]{:S(2)}) copy-start(s32[768]{0:T(1024)S(1)} %convert_add_fusion.1) | copy-start | bytes 9220
  9.5 111.1 %copy-start.22 = (s32[768]{0:T(1024)}, s32[768]{0:T(1024)S(1)}, u32[]{:S(2)}) copy-start(s32[768]{0:T(1024)S(1)} %convert_add_fusion) | copy-start | bytes 9220
  13.1 15.6 %all-to-all-start.3 = ((s32[16,1,128]{2,1,0:T(1,128)}), s32[16,1,128]{2,1,0:T(1,128)S(1)}, u32[]{:S(2)}, u32[]{:S(2)}) async-start(s32[16,1,128]{2,1,0:T(1,128)} %bitcast.29), calls=%async_computation.4 | async-start | bytes 16384 | tf_op jit(solution)/shard_map/all_to_all | solution.py:176
  28.7 16.0 %all-to-all-start = ((s32[16,1,128]{2,1,0:T(1,128)}), s32[16,1,128]{2,1,0:T(1,128)S(1)}, u32[]{:S(2)}, u32[]{:S(2)}) async-start(s32[16,1,128]{2,1,0:T(1,128)} %bitcast), calls=%async_computation | async-start | bytes 16384 | tf_op jit(solution)/shard_map/all_to_all | solution.py:176
  44.7 49.2 %all-to-all-start.4 = ((bf16[16,128,512]{2,1,0:T(8,128)(2,1)}), bf16[16,128,512]{2,1,0:T(8,128)(2,1)}, u32[]{:S(2)}, u32[]{:S(2)}) async-start(bf16[16,128,512]{2,1,0:T(8,128)(2,1)} %select_select_fusion), calls=%async_computation.5 | async-start | bytes 4194304 | tf_op jit(solution)/shard_map/all_to_all | solution.py:177
  93.9 52.5 %all-to-all-start.1 = ((bf16[16,128,512]{2,1,0:T(8,128)(2,1)}), bf16[16,128,512]{2,1,0:T(8,128)(2,1)}, u32[]{:S(2)}, u32[]{:S(2)}) async-start(bf16[16,128,512]{2,1,0:T(8,128)(2,1)} %select_select_fusion.1), calls=%async_computation.1 | async-start | bytes 4194304 | tf_op jit(solution)/shard_map/all_to_all | solution.py:177
  103.8 63.0 %reduce-scatter.5.cloned.1.call-start = ((), (), s32[]{:S(2)}) async-start(), calls=%async_computation.9 | async-start | bytes 393216 | tf_op jit(solution)/shard_map/reduce_scatter | solution.py:73
  110.7 8.3 %copy-start.13 = (s32[1,256]{1,0:T(1,128)}, s32[1,256]{1,0:T(1,128)S(1)}, u32[]{:S(2)}) copy-start(s32[1,256]{1,0:T(1,128)S(1)} %get-tuple-element.67) | copy-start | bytes 3076
  110.7 8.3 %copy-start.15 = (s32[1,256]{1,0:T(1,128)}, s32[1,256]{1,0:T(1,128)S(1)}, u32[]{:S(2)}) copy-start(s32[1,256]{1,0:T(1,128)S(1)} %get-tuple-element.66) | copy-start | bytes 3076
  110.7 8.6 %copy-start.24 = (u32[32]{0:T(128)S(1)}, u32[32]{0:T(128)}, u32[]{:S(2)}) copy-start(u32[32]{0:T(128)} %constant.85) | copy-start | bytes 388
  124.3 22.2 %copy-start.7 = (bf16[768,512]{0,1:T(8,128)(2,1)}, bf16[768,512]{0,1:T(8,128)(2,1)S(1)}, u32[]{:S(2)}) copy-start(bf16[768,512]{0,1:T(8,128)(2,1)S(1)} %fusion.34) | copy-start | bytes 2359300
  124.6 21.9 %copy-start.5 = (bf16[256,4,2,64]{0,3,2,1:T(8,128)(2,1)}, bf16[256,4,2,64]{0,3,2,1:T(8,128)(2,1)S(1)}, u32[]{:S(2)}) copy-start(bf16[256,4,2,64]{0,3,2,1:T(8,128)(2,1)S(1)} %pad_maximum_fusion.5) | copy-start | bytes 786436
  150.1 0.9 copy-start.6
  151.1 18.7 %copy-start.1 = (f32[256,512]{0,1:T(8,128)}, f32[256,512]{0,1:T(8,128)S(1)}, u32[]{:S(2)}) copy-start(f32[256,512]{0,1:T(8,128)S(1)} %get-tuple-element.50) | copy-start | bytes 1572868
  151.1 18.7 %copy-start.2 = (f32[256,512]{0,1:T(8,128)}, f32[256,512]{0,1:T(8,128)S(1)}, u32[]{:S(2)}) copy-start(f32[256,512]{0,1:T(8,128)S(1)} %get-tuple-element.51) | copy-start | bytes 1572868
  151.1 0.8 copy-start.11
  153.9 24.9 %reduce-scatter.3.cloned.1.call-start = ((), (), s32[]{:S(2)}) async-start(), calls=%async_computation.8 | async-start | bytes 393216 | tf_op jit(solution)/shard_map/reduce_scatter | solution.py:73
  174.3 9.1 %copy-start.23 = (s32[768]{0:T(1024)S(1)}, s32[768]{0:T(1024)}, u32[]{:S(2)}) copy-start(s32[768]{0:T(1024)} %copy-done.22) | copy-start | bytes 9220
  187.7 7.9 %copy-start.18 = (f32[2,1,128]{2,1,0:T(1,128)S(1)}, f32[2,1,128]{2,1,0:T(1,128)}, u32[]{:S(2)}) copy-start(f32[2,1,128]{2,1,0:T(1,128)} %convert_element_type.222) | copy-start | bytes 3076
  187.7 69.7 %all-to-all-start.5 = ((bf16[16,128,512]{2,1,0:T(8,128)(2,1)}), bf16[16,128,512]{2,1,0:T(8,128)(2,1)S(1)}, u32[]{:S(2)}, u32[]{:S(2)}) async-start(bf16[16,128,512]{2,1,0:T(8,128)(2,1)} %bitcast.139), calls=%async_computation.7 | async-start | bytes 4194304 | tf_op jit(solution)/shard_map/all_to_all | solution.py:191
  195.2 333.2 %all-reduce.6.cloned.1.call-start = ((), (), s32[]{:S(2)}) async-start(), calls=%async_computation.10 | async-start | bytes 16777216 | tf_op jit(solution)/shard_map/psum | solution.py:197
  195.6 4.9 copy-start.3
  195.6 5.8 %copy-start.8 = (f32[256,512]{0,1:T(8,128)S(1)}, f32[256,512]{0,1:T(8,128)}, u32[]{:S(2)}) copy-start(f32[256,512]{0,1:T(8,128)} %get-tuple-element.69) | copy-start | bytes 1572868
  198.0 3.5 copy-start.9
  198.0 3.5 copy-start.10
  199.4 2.2 copy-start.16
  201.6 4.9 copy-start.14
  213.9 3.9 copy-start.4
  257.4 93.2 %all-to-all-start.2 = ((bf16[16,128,512]{2,1,0:T(8,128)(2,1)}), bf16[16,128,512]{2,1,0:T(8,128)(2,1)}, u32[]{:S(2)}, u32[]{:S(2)}) async-start(bf16[16,128,512]{2,1,0:T(8,128)(2,1)} %bitcast.140), calls=%async_computation.3 | async-start | bytes 4194304 | tf_op jit(solution)/shard_map/all_to_all | solution.py:191
  285.1 9.7 %copy-start.20 = (s32[2048]{0:T(1024)S(1)}, s32[2048]{0:T(1024)}, u32[]{:S(2)}) copy-start(s32[2048]{0:T(1024)} %param.13) | copy-start | bytes 24580
  355.0 2.8 copy-start.12
  357.8 3.0 copy-start
  366.5 169.3 %copy-start.19 = (f32[2048]{0:T(1024)S(1)}, f32[2048]{0:T(1024)}, u32[]{:S(2)}) copy-start(f32[2048]{0:T(1024)} %param.12) | copy-start | bytes 24580
  542.7 5.4 copy-start.17
Sparse Core Ops, SparseCore 0:
  154.1 11.9 reduce-scatter.4
  168.2 10.5 reduce-scatter.2
  214.0 314.2 all-reduce.5
where the time goes:
time: 571 us; the launch traced here: 565 us
  waiting for transfers between devices  307 us (54%)
  starting transfers between devices  64.9 us (11%)
  matrix products  58.9 us (10%)
  other arithmetic  58 us (10%)
  local copies, waits for them, and re-layouts  47.1 us (8%)
  between operations  15.5 us (3%)
  blocking collectives  13.7 us (2%)
    psum x1, waiting for transfers between devices, per_device(): rel_grad = lax.psum(rel_total, 'ent')  162 us
    all_to_all x2, waiting for transfers between devices, per_device(): lax.all_to_all(outgoing, 'ent', split_axis=0, concat_axis=0, tiled=True)  88.1 us
    all_to_all x2, waiting for transfers between devices, per_device(): lax.all_to_all(look_up(received, ent_low, row_base), 'ent', split_axis=0,...  51 us
    all_to_all x2, starting transfers between devices, per_device(): lax.all_to_all(outgoing, 'ent', split_axis=0, concat_axis=0, tiled=True)  35.2 us
    dot_general x10, matrix products, contract_first(): lax.dot_general(former, latter, (((0,), (0,)), ((), ())), preferred_eleme...  27.5 us
    gather x2, local copies, waits for them, and re-layouts, look_up(): jnp.take(ent_low, jnp.clip(local_rows, 0, ent_low.shape[0] - 1), axis=0)  18.4 us
    sub x2, other arithmetic, adagrad(): return table - LEARN_RATE * grad / jnp.sqrt(new_state)[:, None]  16.9 us
    all_to_all x2, starting transfers between devices, per_device(): lax.all_to_all(look_up(received, ent_low, row_base), 'ent', split_axis=0,...  16.8 us
  transfers between devices with their start and end apart: 9, of which 7 were waited for; matrix products, arithmetic and copies ran while one was open for 21% of the time, Pallas kernels for 0%

commit v1 on v0

v1 whole, which is shorter than its diff:
```python
import jax
import jax.numpy as jnp
from jax import lax
from jax.sharding import PartitionSpec as P

RANK = 512
BLK = 64


LEARN_RATE = 0.1
REG_WEIGHT = 0.01


def halves(values):
    shaped = values.reshape(values.shape[:-1] + (values.shape[-1] // (2 * BLK), 2, BLK))
    return (shaped[..., 0, :], shaped[..., 1, :])


def joined(real_part, imag_part):
    stacked = jnp.stack([real_part, imag_part], axis=-2)
    return stacked.reshape(stacked.shape[:-3] + (stacked.shape[-3] * 2 * BLK,))


def complex_product(former, latter):
    former_re, former_im = halves(former)
    latter_re, latter_im = halves(latter)
    return joined(
        former_re * latter_re - former_im * latter_im, former_re * latter_im + former_im * latter_re
    )


def conjugate(values):
    real_part, imag_part = halves(values)
    return joined(real_part, -imag_part)


def rounded(values):
    return lax.optimization_barrier(values.astype(jnp.bfloat16))


def contract_first(former, latter):
    return lax.dot_general(
        former, latter, (((0,), (0,)), ((), ())), preferred_element_type=jnp.float32
    )


def contract_last(former, latter):
    return lax.dot_general(
        former, latter, (((1,), (1,)), ((), ())), preferred_element_type=jnp.float32
    )


def exchange(blocks):
    return [
        lax.all_to_all(block, "ent", split_axis=0, concat_axis=0, tiled=True) for block in blocks
    ]


def group_step(rows_group, rel_float, group_len):
    head_float = rows_group[:group_len].astype(jnp.float32)
    tail_float = rows_group[group_len : 2 * group_len].astype(jnp.float32)
    noise_rows = rows_group[2 * group_len :]
    width_neg = noise_rows.shape[0]
    query = rounded(complex_product(head_float, rel_float))
    probe = rounded(complex_product(conjugate(rel_float), tail_float))
    part_pos = jnp.sum(query.astype(jnp.float32) * tail_float, axis=-1, keepdims=True)
    part = jnp.concatenate(
        [
            contract_last(query, noise_rows),
            contract_last(probe, noise_rows),
            jnp.broadcast_to(part_pos, (group_len, 128)),
        ],
        axis=1,
    ).astype(jnp.bfloat16)
    scores = jnp.sum(lax.all_gather(part, "dim").astype(jnp.float32), axis=0)
    both_coef = rounded(jax.nn.sigmoid(scores[:, : 2 * width_neg]) / width_neg)
    pos_float = -jax.nn.sigmoid(-scores[:, 2 * width_neg : 2 * width_neg + 1])
    pos_float = rounded(pos_float).astype(jnp.float32)
    tail_coef = both_coef[:, :width_neg]
    head_coef = both_coef[:, width_neg:]
    tail_pull = pos_float * tail_float + jnp.dot(
        tail_coef, noise_rows, preferred_element_type=jnp.float32
    )
    head_pull = jnp.dot(head_coef, noise_rows, preferred_element_type=jnp.float32)
    head_side = pos_float * head_float + head_pull
    head_grad = complex_product(conjugate(rel_float), tail_pull).astype(jnp.bfloat16)
    tail_grad = complex_product(rel_float, head_side).astype(jnp.bfloat16)
    noise_grad = (contract_first(tail_coef, query) + contract_first(head_coef, probe)).astype(
        jnp.bfloat16
    )
    rel_grad = complex_product(conjugate(head_float), tail_pull) + complex_product(
        tail_float, conjugate(head_pull)
    )
    return (
        jnp.concatenate([head_grad, tail_grad, noise_grad], axis=0),
        rel_grad.astype(jnp.bfloat16),
    )


def placement_of(wanted_row, owners, rows_here, slot_count):
    request_count = wanted_row.shape[0]
    owner_of = wanted_row // rows_here
    owner_hits = (owner_of[:, None] == jnp.arange(owners, dtype=jnp.int32)[None, :]).astype(
        jnp.bfloat16
    )
    order = jnp.arange(request_count, dtype=jnp.int32)
    earlier = (order[:, None] > order[None, :]).astype(jnp.bfloat16)
    before = jnp.dot(earlier, owner_hits, preferred_element_type=jnp.float32)
    slot_rank = jnp.sum(before * owner_hits.astype(jnp.float32), axis=-1).astype(jnp.int32)
    slot_flat = owner_of * slot_count + slot_rank
    matches = slot_flat[:, None] == jnp.arange(owners * slot_count, dtype=jnp.int32)[None, :]
    slot_ids = jnp.sum(jnp.where(matches, wanted_row[:, None] + 1, 0), axis=0) - 1
    return (matches.astype(jnp.bfloat16), slot_ids.reshape(owners, slot_count))


def accumulate(local_rows, received_rows, totals, counts):
    flat_rows = received_rows.reshape(local_rows.shape[0], received_rows.shape[-1])
    positions = jnp.arange(totals.shape[0], dtype=jnp.int32)
    one_hot = (local_rows[:, None] == positions[None, :]).astype(jnp.bfloat16)
    totals = totals + contract_first(one_hot, flat_rows)
    counts = counts + jnp.sum(one_hot, axis=0, dtype=jnp.float32)
    return (totals, counts)


def adagrad(table, state, grad, squares):
    new_state = state + squares / (2 * RANK)
    scale = LEARN_RATE / jnp.sqrt(new_state)
    return table - grad * scale[:, None]


def per_device(entities, ent_state, buckets, relations, rel_state, triples, negatives):
    owners = lax.axis_size("ent")
    rows_here, columns_here = entities.shape
    rel_count = relations.shape[0]
    row_base = lax.axis_index("ent") * rows_here
    groups_here = negatives.shape[0]
    group_len = triples.shape[1] // groups_here
    request_count = 2 * group_len + negatives.shape[1]
    slot_count = 8 * ((request_count + 3 * owners - 1) // (3 * owners))
    ent_low = entities.astype(jnp.bfloat16)
    head_ids = triples[0].reshape(groups_here, group_len)
    tail_ids = triples[2].reshape(groups_here, group_len)
    wanted = jnp.concatenate([head_ids, tail_ids, negatives], axis=1)
    placed = [
        placement_of(wanted[index], owners, rows_here, slot_count) for index in range(groups_here)
    ]
    slot_ids = jnp.stack([slots for _, slots in placed], axis=1)
    received = lax.all_to_all(slot_ids, "ent", split_axis=0, concat_axis=0, tiled=True)
    local_rows = [received[:, index].reshape(-1) - row_base for index in range(groups_here)]
    looked_up = [
        jnp.take(ent_low, jnp.clip(rows, 0, rows_here - 1), axis=0).reshape(
            owners, slot_count, columns_here
        )
        for rows in local_rows
    ]
    arrived = exchange(looked_up)
    rel_float = rounded(jnp.take(relations, triples[1], axis=0)).astype(jnp.float32)
    outgoing, rel_rows = [], []
    for index in range(groups_here):
        matches = placed[index][0]
        rows_group = jnp.dot(
            matches,
            arrived[index].reshape(owners * slot_count, columns_here),
            preferred_element_type=jnp.float32,
        ).astype(jnp.bfloat16)
        grads, rel_row = group_step(
            rows_group, rel_float[index * group_len : (index + 1) * group_len], group_len
        )
        outgoing.append(
            contract_first(matches, grads)
            .astype(jnp.bfloat16)
            .reshape(owners, slot_count, columns_here)
        )
        rel_rows.append(rel_row)
    rel_hits = (
        triples[1][:, None] == jnp.arange(rel_count, dtype=jnp.int32)[None, :]
    ).astype(jnp.bfloat16)
    rel_part = contract_first(rel_hits, jnp.concatenate(rel_rows, axis=0)).astype(jnp.bfloat16)
    rel_share = lax.psum_scatter(rel_part, "ent", scatter_dimension=0, tiled=True)
    rel_grad = lax.all_gather(rel_share, "ent", axis=0, tiled=True).astype(jnp.float32)
    returned = exchange(outgoing)
    totals = jnp.zeros((rows_here, columns_here), jnp.float32)
    counts = jnp.zeros((rows_here,), jnp.float32)
    for index in range(groups_here):
        totals, counts = accumulate(local_rows[index], returned[index], totals, counts)
    weight = REG_WEIGHT * (buckets.astype(jnp.float32) + 1.0) * counts
    totals = totals + weight[:, None] * 3.0 * entities * jnp.abs(entities)
    ent_squares = jnp.sum(totals * totals, axis=-1)
    ent_all, rel_all = lax.psum((ent_squares, jnp.sum(rel_grad * rel_grad, axis=-1)), "dim")
    new_relations = adagrad(relations, rel_state, rel_grad, rel_all)
    new_entities = adagrad(entities, ent_state, totals, ent_all)
    return (new_entities, new_relations)


def solution(mesh):
    placed = (
        P("ent", "dim"),
        P("ent"),
        P("ent"),
        P(None, "dim"),
        P(),
        P(None, "ent"),
        P("ent", None),
    )
    return jax.shard_map(
        per_device,
        mesh=mesh,
        in_specs=placed,
        out_specs=(P("ent", "dim"), P(None, "dim")),
        check_vma=False,
    )
```

time: 571 us -> 432 us (0.76)
  waiting for transfers between devices: 307 us -> 227 us
  starting transfers between devices: 64.9 us -> 38.2 us
  other arithmetic: 58 us -> 41.7 us
  matrix products: 58.9 us -> 48.4 us
    psum x1 -> x0, waiting for transfers between devices: 162 us -> none  [per_device(): rel_grad = lax.psum(rel_total, 'ent')]
    reduce_scatter x2 -> x1, waiting for transfers between devices: 2.49 us -> 113 us  [per_device(): lax.psum_scatter(rel_part, 'ent', scatter_dimension=0, tiled=True)]
    all_to_all x4, waiting for transfers between devices: 139 us -> 90.5 us  [exchange(): lax.all_to_all(block, 'ent', split_axis=0, concat_axis=0, tiled=True)]
    all_to_all x4, starting transfers between devices: 52 us -> 29.8 us  [exchange(): lax.all_to_all(block, 'ent', split_axis=0, concat_axis=0, tiled=True)]
    all_gather x0 -> x1, waiting for transfers between devices: none -> 18.7 us  [per_device(): lax.all_gather(rel_share, 'ent', axis=0, tiled=True).astype(jnp.float32)]
    dot_general x4 -> x2, matrix products: 19.6 us -> 7.39 us  [per_device(): jnp.dot(matches, arrived[index].reshape(owners * slot_count, columns_here...]
    convert_element_type x3 -> x2, other arithmetic: 7.08 us -> 0.16 us  [group_step(): rel_grad.astype(jnp.bfloat16)]
    dot_general x10 -> x9, matrix products: 27.5 us -> 33.4 us  [contract_first(): lax.dot_general(former, latter, (((0,), (0,)), ((), ())), preferred_eleme...]
  transfers between devices with their start and end apart: 9 -> 7, of which waited for: 7 -> 6; matrix products, arithmetic and copies ran while one was open for 21% -> 17% of each run, Pallas kernels for 0% -> 0%
where the time goes in v1:
time: 432 us; the launch traced here: 424 us
  waiting for transfers between devices  227 us (53%)
  matrix products  48.4 us (11%)
  local copies, waits for them, and re-layouts  44.8 us (10%)
  other arithmetic  41.7 us (10%)
  starting transfers between devices  38.2 us (9%)
  between operations  15.2 us (4%)
  blocking collectives  8.54 us (2%)
    reduce_scatter x1, waiting for transfers between devices, per_device(): lax.psum_scatter(rel_part, 'ent', scatter_dimension=0, tiled=True)  113 us
    all_to_all x4, waiting for transfers between devices, exchange(): lax.all_to_all(block, 'ent', split_axis=0, concat_axis=0, tiled=True)  90.5 us
    dot_general x9, matrix products, contract_first(): lax.dot_general(former, latter, (((0,), (0,)), ((), ())), preferred_eleme...  33.4 us
    all_to_all x4, starting transfers between devices, exchange(): lax.all_to_all(block, 'ent', split_axis=0, concat_axis=0, tiled=True)  29.8 us
    all_gather x1, waiting for transfers between devices, per_device(): lax.all_gather(rel_share, 'ent', axis=0, tiled=True).astype(jnp.float32)  18.7 us
    gather x2, local copies, waits for them, and re-layouts, per_device(): jnp.take(ent_low, jnp.clip(rows, 0, rows_here - 1), axis=0)  18.4 us
    sub x2, other arithmetic, adagrad(): return table - grad * scale[:, None]  14.6 us
    unnamed x54, local copies, waits for them, and re-layouts  14.6 us
  transfers between devices with their start and end apart: 7, of which 6 were waited for; matrix products, arithmetic and copies ran while one was open for 17% of the time, Pallas kernels for 0%

profile of v1, /device:TPU:0, one launch (start us, length us, event | category | flops | bytes accessed | tf_op | source)
XLA Modules:
  0.0 424.4 jit_solution(8799744945047041162)
XLA Ops:
  7.2 0.8 slice_reduce_fusion.2
  8.1 0.7 constant_dynamic-update-slice_fusion
  8.8 0.3 fusion.33
  9.2 0.9 select_reduce_fusion
  10.0 0.3 fusion.34
  10.4 0.9 select_reduce_fusion.1
  11.3 0.6 pad_add_fusion
  11.9 8.3 %all-to-all-start = ((s32[16,2,128]{2,1,0:T(2,128)}), s32[16,2,128]{2,1,0:T(2,128)S(1)}, u32[]{:S(2)}, u32[]{:S(2)}) async-start(s32[16,2,128]{2,1,0:T(2,128)} %pad_add_fusion), calls=%async_computation | async-start | bytes 32768 | tf_op jit(solution)/shard_map/all_to_all | solution.py:148
  20.3 2.5 convert_element_type.185
  22.8 4.9 %all-to-all-done = s32[16,2,128]{2,1,0:T(2,128)S(1)} async-done(((s32[16,2,128]{2,1,0:T(2,128)}), s32[16,2,128]{2,1,0:T(2,128)S(1)}, u32[]{:S(2)}, u32[]{:S(2)}) %all-to-all-start) | async-done | bytes 16416 | tf_op jit(solution)/shard_map/all_to_all | solution.py:148
  27.7 9.2 %gather_fusion.2 = bf16[2048,512]{1,0:T(8,128)(2,1)} fusion(bf16[2048,512]{1,0:T(8,128)(2,1)S(1)} %convert_element_type.185, s32[2048]{0:T(1024)S(1)} %fusion.85), kind=kCustom, calls=%fused_computation.1.clone | custom fusion | bytes 4202496 | tf_op jit(solution)/shard_map/jit(_take)/gather | solution.py:151
  36.9 2.7 broadcast_select_fusion
  39.6 4.4 %all-to-all-start.3 = ((bf16[16,128,512]{2,1,0:T(8,128)(2,1)}), bf16[16,128,512]{2,1,0:T(8,128)(2,1)}, u32[]{:S(2)}, u32[]{:S(2)}) async-start(bf16[16,128,512]{2,1,0:T(8,128)(2,1)} %bitcast.60), calls=%async_computation.3 | async-start | bytes 4194304 | tf_op jit(solution)/shard_map/all_to_all | solution.py:55
  44.1 9.2 %gather_fusion.1 = bf16[2048,512]{1,0:T(8,128)(2,1)} fusion(bf16[2048,512]{1,0:T(8,128)(2,1)S(1)} %convert_element_type.185, s32[2048]{0:T(1024)S(1)} %fusion.84), kind=kCustom, calls=%fused_computation.clone | custom fusion | bytes 4202496 | tf_op jit(solution)/shard_map/jit(_take)/gather | solution.py:151
  53.3 2.8 broadcast_select_fusion.1
  56.1 30.3 %all-to-all-done.3 = bf16[16,128,512]{2,1,0:T(8,128)(2,1)} async-done(((bf16[16,128,512]{2,1,0:T(8,128)(2,1)}), bf16[16,128,512]{2,1,0:T(8,128)(2,1)}, u32[]{:S(2)}, u32[]{:S(2)}) %all-to-all-start.3) | async-done | bytes 2097184 | tf_op jit(solution)/shard_map/all_to_all | solution.py:55
  86.3 9.8 %all-to-all-start.1 = ((bf16[16,128,512]{2,1,0:T(8,128)(2,1)}), bf16[16,128,512]{2,1,0:T(8,128)(2,1)}, u32[]{:S(2)}, u32[]{:S(2)}) async-start(bf16[16,128,512]{2,1,0:T(8,128)(2,1)} %bitcast.7), calls=%async_computation.1 | async-start | bytes 4194304 | tf_op jit(solution)/shard_map/all_to_all | solution.py:55
  96.2 0.7 compare_select_fusion.2
  96.9 5.4 %gather_fusion = bf16[512,512]{1,0:T(8,128)(2,1)S(1)} fusion(f32[4096,512]{1,0:T(8,128)} %param.12, s32[1024]{0:T(1024)S(1)} %pad_clamp_fusion), kind=kCustom, calls=%fused_computation.2 | custom fusion | bytes 1050624 | tf_op jit(solution)/shard_map/jit(_take)/gather | solution.py:157
  103.0 3.7 fusion.24
  107.2 0.3 fusion.29
  107.5 0.3 fusion.30
  107.8 0.7 pad_maximum_fusion.1
  108.5 1.9 copy.117
  110.4 2.6 all_gather.12
  113.1 0.8 copy-done.3
  114.0 0.7 copy.134
  114.6 1.2 fusion.59
  115.8 0.7 negate_convert_fusion
  116.5 1.1 convolution_add_fusion.1
  117.6 1.2 multiply_add_fusion.1
  118.9 19.9 %all-to-all-done.1 = bf16[16,128,512]{2,1,0:T(8,128)(2,1)} async-done(((bf16[16,128,512]{2,1,0:T(8,128)(2,1)}), bf16[16,128,512]{2,1,0:T(8,128)(2,1)}, u32[]{:S(2)}, u32[]{:S(2)}) %all-to-all-start.1) | async-done | bytes 2097184 | tf_op jit(solution)/shard_map/all_to_all | solution.py:55
  138.8 3.7 fusion.23
  142.9 0.3 fusion.27
  143.7 0.3 copy-done.9
  144.0 0.7 pad_maximum_fusion
  144.7 1.9 copy.110
  146.6 2.5 all_gather.11
  149.2 0.9 fusion.58
  150.0 0.6 copy.133
  150.7 0.7 negate_convert_fusion.1
  151.4 1.4 convolution_add_fusion.3
  152.8 2.2 multiply_add_fusion.2
  155.0 1.1 multiply_subtract_fusion.1
  156.1 0.8 multiply_subtract_fusion.2
  157.3 4.6 %convolution_convert_fusion = bf16[4096,512]{1,0:T(8,128)(2,1)} fusion(s32[512]{0:T(512)S(1)} %bitcast.114, bf16[256,512]{0,1:T(8,128)(2,1)S(1)} %bitcast.96, bf16[256,512]{0,1:T(8,128)(2,1)S(1)} %bitcast.97), kind=kOutput, calls=%fused_computation.27 | convolution fusion | flops 2154823680 | bytes 4720640 | tf_op jit(solution)/shard_map/dot_general | solution.py:42
  161.9 1.0 copy-done.11
  164.0 3.3 fusion.20
  167.3 9.8 %all-to-all-start.4 = ((bf16[16,128,512]{2,1,0:T(8,128)(2,1)}), bf16[16,128,512]{2,1,0:T(8,128)(2,1)}, u32[]{:S(2)}, u32[]{:S(2)}) async-start(bf16[16,128,512]{2,1,0:T(8,128)(2,1)} %bitcast.37), calls=%async_computation.4 | async-start | bytes 4194304 | tf_op jit(solution)/shard_map/all_to_all | solution.py:55
  177.2 113.4 %reduce-scatter.2.cloned.1.call-done = bf16[256,512]{1,0:T(8,128)(2,1)} async-done(((bf16[4096,512]{1,0:T(8,128)(2,1)}), bf16[256,512]{1,0:T(8,128)(2,1)}) %reduce-scatter.2.cloned.1.call-update) | async-done | bytes 262160 | tf_op jit(solution)/shard_map/reduce_scatter | solution.py:179
  291.7 3.4 fusion.19
  295.1 5.7 %all-to-all-start.2 = ((bf16[16,128,512]{2,1,0:T(8,128)(2,1)}), bf16[16,128,512]{2,1,0:T(8,128)(2,1)S(1)}, u32[]{:S(2)}, u32[]{:S(2)}) async-start(bf16[16,128,512]{2,1,0:T(8,128)(2,1)} %bitcast.20), calls=%async_computation.2 | async-start | bytes 4194304 | tf_op jit(solution)/shard_map/all_to_all | solution.py:55
  300.9 5.6 %copy.125 = f32[2048,512]{0,1:T(8,128)} copy(f32[2048,512]{1,0:T(8,128)} %param.9) | data formatting | bytes 8388608 | tf_op args[0]
  306.5 2.1 convert_reduce_fusion
  308.5 2.1 convert_reduce_fusion.1
  310.6 8.8 %fusion.1 = f32[2048,512]{0,1:T(8,128)} fusion(bf16[2048,512]{1,0:T(8,128)(2,1)} %bitcast.38, s32[2048]{0:T(1024)S(1)} %bitcast.105), kind=kOutput, calls=%fused_computation.7 | convolution fusion | flops 4299161600 | bytes 6299648 | tf_op jit(solution)/shard_map/dot_general | solution.py:42
  319.4 40.3 %all-to-all-done.2 = bf16[16,128,512]{2,1,0:T(8,128)(2,1)S(1)} async-done(((bf16[16,128,512]{2,1,0:T(8,128)(2,1)}), bf16[16,128,512]{2,1,0:T(8,128)(2,1)S(1)}, u32[]{:S(2)}, u32[]{:S(2)}) %all-to-all-start.2) | async-done | bytes 2097184 | tf_op jit(solution)/shard_map/all_to_all | solution.py:55
  359.7 12.3 %multiply_reduce_fusion = (f32[2048]{0:T(1024)S(1)}, f32[2048,512]{0,1:T(8,128)}) fusion(f32[2048,512]{0,1:T(8,128)} %copy.125, f32[2048]{0:T(1024)S(1)} %multiply_multiply_fusion, f32[2048,512]{0,1:T(8,128)} %fusion.1, bf16[2048,512]{1,0:T(8,128)(2,1)S(1)} %bitcast.87, s32[2048]{0:T(1024)S(1)} %bitcast.101), kind=kOutput, calls=%fused_computation.30 | convolution fusion | flops 4306499584 | bytes 14704640 | tf_op jit(solution)/shard_map/dot_general | solution.py:42
  371.9 18.7 %all-gather.2.cloned.1.call-done = bf16[4096,512]{1,0:T(8,128)(2,1)} async-done(((bf16[256,512]{1,0:T(8,128)(2,1)}), bf16[4096,512]{1,0:T(8,128)(2,1)}) %all-gather.2.cloned.1.call-update) | async-done | bytes 4194320 | tf_op jit(solution)/shard_map/all_gather | solution.py:180
  390.6 3.1 fusion.4
  393.7 3.4 all-reduce
  397.2 6.7 %multiply_subtract_fusion = f32[2048,512]{0,1:T(8,128)} fusion(f32[2048,512]{0,1:T(8,128)} %copy.125, f32[2048,512]{0,1:T(8,128)} %get-tuple-element.73, f32[2048]{0:T(1024)S(1)} %rsqrt_multiply_fusion.1), kind=kLoop, calls=%fused_computation.29 | loop fusion | flops 2097152 | bytes 12591104 | tf_op jit(solution)/shard_map/sub | solution.py:128
  403.9 5.3 %copy.128 = f32[2048,512]{1,0:T(8,128)} copy(f32[2048,512]{0,1:T(8,128)} %multiply_subtract_fusion) | data formatting | bytes 8388608
  409.3 7.9 %fusion.5 = f32[4096,512]{1,0:T(8,128)} fusion(f32[4096,512]{1,0:T(8,128)} %param.12, bf16[4096,512]{1,0:T(8,128)(2,1)} %all-gather.2.cloned.1.call-done, f32[4096]{0:T(1024)S(1)} %rsqrt_multiply_fusion), kind=kLoop, calls=%fused_computation.14 | loop fusion | flops 6291456 | bytes 20987904 | tf_op jit(solution)/shard_map/sub | solution.py:128
  (111 shorter events, 4.8 us)
Async XLA Ops:
  8.0 94.3 %copy-start.17 = (s32[1,512]{1,0:T(1,128)}, s32[1,512]{1,0:T(1,128)S(1)}, u32[]{:S(2)}) copy-start(s32[1,512]{1,0:T(1,128)S(1)} %get-tuple-element.63) | copy-start | bytes 6148
  9.2 93.9 %copy-start.22 = (s32[768]{0:T(1024)}, s32[768]{0:T(1024)S(1)}, u32[]{:S(2)}) copy-start(s32[768]{0:T(1024)S(1)} %get-tuple-element.67) | copy-start | bytes 9220
  10.4 0.9 copy-start.20
  11.9 15.7 %all-to-all-start = ((s32[16,2,128]{2,1,0:T(2,128)}), s32[16,2,128]{2,1,0:T(2,128)S(1)}, u32[]{:S(2)}, u32[]{:S(2)}) async-start(s32[16,2,128]{2,1,0:T(2,128)} %pad_add_fusion), calls=%async_computation | async-start | bytes 32768 | tf_op jit(solution)/shard_map/all_to_all | solution.py:148
  39.6 46.7 %all-to-all-start.3 = ((bf16[16,128,512]{2,1,0:T(8,128)(2,1)}), bf16[16,128,512]{2,1,0:T(8,128)(2,1)}, u32[]{:S(2)}, u32[]{:S(2)}) async-start(bf16[16,128,512]{2,1,0:T(8,128)(2,1)} %bitcast.60), calls=%async_computation.3 | async-start | bytes 4194304 | tf_op jit(solution)/shard_map/all_to_all | solution.py:55
  86.3 52.5 %all-to-all-start.1 = ((bf16[16,128,512]{2,1,0:T(8,128)(2,1)}), bf16[16,128,512]{2,1,0:T(8,128)(2,1)}, u32[]{:S(2)}, u32[]{:S(2)}) async-start(bf16[16,128,512]{2,1,0:T(8,128)(2,1)} %bitcast.7), calls=%async_computation.1 | async-start | bytes 4194304 | tf_op jit(solution)/shard_map/all_to_all | solution.py:55
  96.1 194.5 %reduce-scatter.2.cloned.1.call-start = ((), (), s32[]{:S(2)}) async-start(), calls=%async_computation.6 | async-start | bytes 4456448 | tf_op jit(solution)/shard_map/reduce_scatter | solution.py:179
  107.0 6.9 %copy-start.7 = (bf16[256,4,2,64]{0,3,2,1:T(8,128)(2,1)}, bf16[256,4,2,64]{0,3,2,1:T(8,128)(2,1)S(1)}, u32[]{:S(2)}) copy-start(bf16[256,4,2,64]{0,3,2,1:T(8,128)(2,1)S(1)} %pad_maximum_fusion.7) | copy-start | bytes 786436
  107.1 11.8 %copy-start.1 = (bf16[256,4,2,64]{0,3,2,1:T(8,128)(2,1)}, bf16[256,4,2,64]{0,3,2,1:T(8,128)(2,1)S(1)}, u32[]{:S(2)}) copy-start(bf16[256,4,2,64]{0,3,2,1:T(8,128)(2,1)S(1)} %pad_maximum_fusion.6) | copy-start | bytes 786436
  113.1 0.8 copy-start.3
  115.8 23.0 %copy-start.4 = (bf16[256,512]{1,0:T(8,128)(2,1)}, bf16[256,512]{1,0:T(8,128)(2,1)S(1)}, u32[]{:S(2)}) copy-start(bf16[256,512]{1,0:T(8,128)(2,1)S(1)} %fusion.59) | copy-start | bytes 786436
  142.5 0.9 copy-start
  143.2 0.7 copy-start.9
  150.7 5.4 %copy-start.13 = (f32[256,512]{0,1:T(8,128)S(1)}, f32[256,512]{0,1:T(8,128)}, u32[]{:S(2)}) copy-start(f32[256,512]{0,1:T(8,128)} %convolution_add_fusion.1) | copy-start | bytes 1572868
  156.1 1.2 copy-start.18
  161.9 1.0 copy-start.11
  161.9 1.3 copy-start.14
  161.9 1.5 copy-start.2
  161.9 1.5 copy-start.5
  161.9 1.8 copy-start.8
  161.9 2.1 copy-start.23
  167.3 123.4 %copy-start.12 = (f32[256,512]{0,1:T(8,128)S(1)}, f32[256,512]{0,1:T(8,128)}, u32[]{:S(2)}) copy-start(f32[256,512]{0,1:T(8,128)} %get-tuple-element.70) | copy-start | bytes 1572868
  167.3 123.8 %copy-start.6 = (bf16[256,512]{1,0:T(8,128)(2,1)S(1)}, bf16[256,512]{1,0:T(8,128)(2,1)}, u32[]{:S(2)}) copy-start(bf16[256,512]{1,0:T(8,128)(2,1)} %fusion.58) | copy-start | bytes 786436
  167.3 124.1 %copy-start.10 = (bf16[256,4,2,64]{0,3,2,1:T(8,128)(2,1)S(1)}, bf16[256,4,2,64]{0,3,2,1:T(8,128)(2,1)}, u32[]{:S(2)}) copy-start(bf16[256,4,2,64]{0,3,2,1:T(8,128)(2,1)} %copy-done.9) | copy-start | bytes 786436
  167.3 124.4 %copy-start.21 = (s32[768]{0:T(1024)S(1)}, s32[768]{0:T(1024)}, u32[]{:S(2)}) copy-start(s32[768]{0:T(1024)} %copy-done.20) | copy-start | bytes 9220
  167.3 127.8 %all-to-all-start.4 = ((bf16[16,128,512]{2,1,0:T(8,128)(2,1)}), bf16[16,128,512]{2,1,0:T(8,128)(2,1)}, u32[]{:S(2)}, u32[]{:S(2)}) async-start(bf16[16,128,512]{2,1,0:T(8,128)(2,1)} %bitcast.37), calls=%async_computation.4 | async-start | bytes 4194304 | tf_op jit(solution)/shard_map/all_to_all | solution.py:55
  177.1 213.5 %all-gather.2.cloned.1.call-start = ((), (), s32[]{:S(2)}) async-start(), calls=%async_computation.7 | async-start | bytes 4456448 | tf_op jit(solution)/shard_map/all_gather | solution.py:180
  295.1 64.6 %all-to-all-start.2 = ((bf16[16,128,512]{2,1,0:T(8,128)(2,1)}), bf16[16,128,512]{2,1,0:T(8,128)(2,1)S(1)}, u32[]{:S(2)}, u32[]{:S(2)}) async-start(bf16[16,128,512]{2,1,0:T(8,128)(2,1)} %bitcast.20), calls=%async_computation.2 | async-start | bytes 4194304 | tf_op jit(solution)/shard_map/all_to_all | solution.py:55
  300.8 9.8 %copy-start.19 = (s32[2048]{0:T(1024)S(1)}, s32[2048]{0:T(1024)}, u32[]{:S(2)}) copy-start(s32[2048]{0:T(1024)} %param.11) | copy-start | bytes 24580
  371.9 25.2 %copy-start.16 = (f32[2048]{0:T(1024)S(1)}, f32[2048]{0:T(1024)}, u32[]{:S(2)}) copy-start(f32[2048]{0:T(1024)} %param.10) | copy-start | bytes 24580
  403.9 5.4 %copy-start.15 = (f32[4096]{0:T(1024)S(1)}, f32[4096]{0:T(1024)}, u32[]{:S(2)}) copy-start(f32[4096]{0:T(1024)} %param.13) | copy-start | bytes 49156
Sparse Core Ops, SparseCore 0:
  162.1 128.5 reduce-scatter.1
  293.4 97.1 all-gather.1

commit v2 on v1

--- a/solution.py
+++ b/solution.py
@@ -122,6 +122,35 @@
     return (totals, counts)
 
 
+def teams(owners):
+    near_size = 4 if owners % 4 == 0 else 1
+    far_size = owners // near_size
+    near = [[row * near_size + place for place in range(near_size)] for row in range(far_size)]
+    far = [[row * near_size + place for row in range(far_size)] for place in range(near_size)]
+    return (near, far)
+
+
+def sum_relations(rel_rows, near_ids, rel_count, near, far):
+    near_size, far_size = len(far), len(near)
+    row_count, columns = rel_rows.shape
+    tiles = rel_rows.reshape(row_count, near_size, columns // near_size).transpose(1, 0, 2)
+    tiles = lax.all_to_all(
+        tiles, "ent", split_axis=0, concat_axis=0, axis_index_groups=near, tiled=True
+    )
+    hits = (near_ids[:, None] == jnp.arange(rel_count, dtype=jnp.int32)[None, :]).astype(
+        jnp.bfloat16
+    )
+    part = contract_first(hits, tiles.reshape(near_size * row_count, columns // near_size)).astype(
+        jnp.bfloat16
+    )
+    share = lax.psum_scatter(
+        part, "ent", scatter_dimension=0, axis_index_groups=far, tiled=True
+    )
+    whole = lax.all_gather(share, "ent", axis=0)
+    whole = whole.reshape(far_size, near_size, rel_count // far_size, columns // near_size)
+    return whole.transpose(0, 2, 1, 3).reshape(rel_count, columns).astype(jnp.float32)
+
+
 def adagrad(table, state, grad, squares):
     new_state = state + squares / (2 * RANK)
     scale = LEARN_RATE / jnp.sqrt(new_state)
@@ -144,17 +173,19 @@
     placed = [
         placement_of(wanted[index], owners, rows_here, slot_count) for index in range(groups_here)
     ]
+    near, far = teams(owners)
+    near_ids = lax.all_gather(triples[1], "ent", axis_index_groups=near, tiled=True)
     slot_ids = jnp.stack([slots for _, slots in placed], axis=1)
     received = lax.all_to_all(slot_ids, "ent", split_axis=0, concat_axis=0, tiled=True)
     local_rows = [received[:, index].reshape(-1) - row_base for index in range(groups_here)]
     looked_up = [
-        jnp.take(ent_low, jnp.clip(rows, 0, rows_here - 1), axis=0).reshape(
+        jnp.take(ent_low, rows, axis=0, mode="clip").reshape(
             owners, slot_count, columns_here
         )
         for rows in local_rows
     ]
     arrived = exchange(looked_up)
-    rel_float = rounded(jnp.take(relations, triples[1], axis=0)).astype(jnp.float32)
+    rel_float = rounded(jnp.take(relations, triples[1], axis=0, mode="clip")).astype(jnp.float32)
     outgoing, rel_rows = [], []
     for index in range(groups_here):
         matches = placed[index][0]
@@ -166,18 +197,16 @@
         grads, rel_row = group_step(
             rows_group, rel_float[index * group_len : (index + 1) * group_len], group_len
         )
-        outgoing.append(
+        sent = (
             contract_first(matches, grads)
             .astype(jnp.bfloat16)
             .reshape(owners, slot_count, columns_here)
         )
+        if index + 1 < groups_here:
+            sent, arrived[index + 1] = lax.optimization_barrier((sent, arrived[index + 1]))
+        outgoing.append(sent)
         rel_rows.append(rel_row)
-    rel_hits = (
-        triples[1][:, None] == jnp.arange(rel_count, dtype=jnp.int32)[None, :]
-    ).astype(jnp.bfloat16)
-    rel_part = contract_first(rel_hits, jnp.concatenate(rel_rows, axis=0)).astype(jnp.bfloat16)
-    rel_share = lax.psum_scatter(rel_part, "ent", scatter_dimension=0, tiled=True)
-    rel_grad = lax.all_gather(rel_share, "ent", axis=0, tiled=True).astype(jnp.float32)
+    rel_grad = sum_relations(jnp.concatenate(rel_rows, axis=0), near_ids, rel_count, near, far)
     returned = exchange(outgoing)
     totals = jnp.zeros((rows_here, columns_here), jnp.float32)
     counts = jnp.zeros((rows_here,), jnp.float32)

time: 432 us -> 416 us (0.963)
  the two profiles are of different devices: /device:TPU:0 before, /device:TPU:13 now
where the time goes in v2:
time: 416 us; the launch traced here: 409 us
  waiting for transfers between devices  189 us (45%)
  local copies, waits for them, and re-layouts  58.8 us (14%)
  matrix products  50.1 us (12%)
  other arithmetic  45.8 us (11%)
  starting transfers between devices  30.4 us (7%)
  blocking collectives  20.4 us (5%)
  between operations  14.8 us (4%)
    all_to_all x4, waiting for transfers between devices, exchange(): lax.all_to_all(block, 'ent', split_axis=0, concat_axis=0, tiled=True)  148 us
    dot_general x9, matrix products, contract_first(): lax.dot_general(former, latter, (((0,), (0,)), ((), ())), preferred_eleme...  37.3 us
    reduce_scatter x1, waiting for transfers between devices, sum_relations(): lax.psum_scatter(part, 'ent', scatter_dimension=0, axis_index_groups=far,...  33 us
    all_to_all x4, starting transfers between devices, exchange(): lax.all_to_all(block, 'ent', split_axis=0, concat_axis=0, tiled=True)  20.1 us
    gather x2, local copies, waits for them, and re-layouts, per_device(): jnp.take(ent_low, rows, axis=0, mode='clip')  18.4 us
    sub x2, other arithmetic, adagrad(): return table - grad * scale[:, None]  16.3 us
    unnamed x35, local copies, waits for them, and re-layouts  12.9 us
    convert_element_type x1, local copies, waits for them, and re-layouts, sum_relations(): whole.transpose(0, 2, 1, 3).reshape(rel_count, columns).astype(jnp.float32)  12 us
  transfers between devices with their start and end apart: 8, of which 7 were waited for; matrix products, arithmetic and copies ran while one was open for 17% of the time, Pallas kernels for 0%

profile of v2, /device:TPU:13, one launch (start us, length us, event | category | flops | bytes accessed | tf_op | source)
XLA Modules:
  0.0 409.4 jit_solution(17636354440529703122)
XLA Ops:
  7.2 0.8 slice_reduce_fusion.2
  8.0 0.7 constant_dynamic-update-slice_fusion
  8.8 0.3 fusion.32
  9.2 0.9 select_reduce_fusion
  10.4 0.9 select_reduce_fusion.1
  11.3 0.6 pad_add_fusion
  11.9 6.6 %all-to-all-start = ((s32[16,2,128]{2,1,0:T(2,128)}), s32[16,2,128]{2,1,0:T(2,128)S(1)}, u32[]{:S(2)}, u32[]{:S(2)}) async-start(s32[16,2,128]{2,1,0:T(2,128)} %pad_add_fusion), calls=%async_computation | async-start | bytes 32768 | tf_op jit(solution)/shard_map/all_to_all | solution.py:179
  18.5 2.5 convert_element_type.201
  21.0 1.8 all-to-all-done
  22.8 9.2 %gather_fusion.1 = bf16[2048,512]{1,0:T(8,128)(2,1)} fusion(bf16[2048,512]{1,0:T(8,128)(2,1)S(1)} %convert_element_type.201, s32[2048]{0:T(1024)S(1)} %broadcast_clamp_fusion.1), kind=kCustom, calls=%fused_computation.1 | custom fusion | bytes 4202496 | tf_op jit(solution)/shard_map/jit(_take)/gather | solution.py:182
  32.0 6.2 %all-to-all-start.1 = ((bf16[16,128,512]{2,1,0:T(8,128)(2,1)}), bf16[16,128,512]{2,1,0:T(8,128)(2,1)}, u32[]{:S(2)}, u32[]{:S(2)}) async-start(bf16[16,128,512]{2,1,0:T(8,128)(2,1)} %bitcast.78), calls=%async_computation.1 | async-start | bytes 4194304 | tf_op jit(solution)/shard_map/all_to_all | solution.py:55
  38.3 5.4 %gather_fusion = bf16[512,512]{1,0:T(8,128)(2,1)S(1)} fusion(f32[4096,512]{1,0:T(8,128)} %param.10, s32[1024]{0:T(1024)S(1)} %pad_clamp_fusion), kind=kCustom, calls=%fused_computation | custom fusion | bytes 1050624 | tf_op jit(solution)/shard_map/jit(_take)/gather | solution.py:188
  43.6 0.9 fusion.86
  44.8 1.2 copy.125
  46.0 7.1 %all-gather = s32[1,2048]{1,0:T(1,128)} all-gather(s32[1,512]{1,0:T(1,128)S(1)} %get-tuple-element.66), channel_id=2, replica_groups={{0,2,4,6},{8,10,12,14},{16,18,20,22},{24,26,28,30},{1,3,5,7},{9,11,13,1..., dimensions={1}, use_global_device_ids=true | all-gather | bytes 10240 | tf_op jit(solution)/shard_map/all_gather | solution.py:177
  53.1 9.2 %gather_fusion.2 = bf16[2048,512]{1,0:T(8,128)(2,1)} fusion(bf16[2048,512]{1,0:T(8,128)(2,1)S(1)} %convert_element_type.201, s32[2048]{0:T(1024)S(1)} %broadcast_clamp_fusion), kind=kCustom, calls=%fused_computation.2 | custom fusion | bytes 4202496 | tf_op jit(solution)/shard_map/jit(_take)/gather | solution.py:182
  62.4 24.3 %all-to-all-done.1 = bf16[16,128,512]{2,1,0:T(8,128)(2,1)} async-done(((bf16[16,128,512]{2,1,0:T(8,128)(2,1)}), bf16[16,128,512]{2,1,0:T(8,128)(2,1)}, u32[]{:S(2)}, u32[]{:S(2)}) %all-to-all-start.1) | async-done | bytes 2097184 | tf_op jit(solution)/shard_map/all_to_all | solution.py:55
  86.7 4.3 %all-to-all-start.2 = ((bf16[16,128,512]{2,1,0:T(8,128)(2,1)}), bf16[16,128,512]{2,1,0:T(8,128)(2,1)}, u32[]{:S(2)}, u32[]{:S(2)}) async-start(bf16[16,128,512]{2,1,0:T(8,128)(2,1)} %bitcast.77), calls=%async_computation.2 | async-start | bytes 4194304 | tf_op jit(solution)/shard_map/all_to_all | solution.py:55
  91.0 3.7 fusion.22
  96.1 0.9 copy.126
  97.0 4.3 %all_gather.17 = bf16[2,256,640]{2,1,0:T(8,128)(2,1)S(1)} all-gather(bf16[1,256,640]{2,1,0:T(8,128)(2,1)} %copy.126), channel_id=1, replica_groups=mesh['ent'=16,'dim'=2] {'dim'}, dimensions={0}, use_global_device_ids=true | all-gather | bytes 983040 | tf_op jit(solution)/shard_map/all_gather | solution.py:75
  101.4 0.8 copy-done
  102.3 1.2 fusion.54
  103.5 1.1 multiply_add_fusion.2
  104.7 0.7 pad_maximum_fusion.5
  105.4 1.8 copy.131
  107.5 0.9 multiply_subtract_fusion.4
  109.2 3.4 fusion.18
  112.5 26.7 %all-to-all-done.2 = bf16[16,128,512]{2,1,0:T(8,128)(2,1)} async-done(((bf16[16,128,512]{2,1,0:T(8,128)(2,1)}), bf16[16,128,512]{2,1,0:T(8,128)(2,1)}, u32[]{:S(2)}, u32[]{:S(2)}) %all-to-all-start.2) | async-done | bytes 2097184 | tf_op jit(solution)/shard_map/all_to_all | solution.py:55
  139.2 3.7 fusion.23
  143.9 0.7 pad_maximum_fusion.1
  144.6 1.9 copy.133
  146.5 3.5 all_gather.18
  150.3 0.6 copy.153
  150.9 0.7 negate_convert_fusion
  151.6 1.1 convolution_add_fusion.1
  152.7 1.2 multiply_add_fusion.1
  153.9 1.2 multiply_subtract_fusion.3
  155.1 1.1 fusion.52
  156.4 1.1 subtract_convert_fusion
  157.5 0.9 copy.138
  158.5 1.2 multiply_subtract_fusion.2
  160.0 0.8 maximum_bitcast_fusion
  160.8 3.5 all-to-all-start.5
  165.2 5.9 %all-to-all-done.5 = bf16[4,512,128]{2,1,0:T(8,128)(2,1)S(1)} async-done(((bf16[4,512,128]{2,1,0:T(8,128)(2,1)}), bf16[4,512,128]{2,1,0:T(8,128)(2,1)S(1)}, u32[]{:S(2)}, u32[]{:S(2)}) %all-to-all-start.5) | async-done | bytes 524320 | tf_op jit(solution)/shard_map/all_to_all | solution.py:137
  171.2 10.2 %fusion.13 = bf16[4096,128]{1,0:T(8,128)(2,1)} fusion(bf16[2048,128]{1,0:T(8,128)(2,1)S(1)} %bitcast.117, s32[2048]{0:T(1024)S(1)} %bitcast.133), kind=kOutput, calls=%fused_computation.27 | convolution fusion | flops 2156396544 | bytes 1581056 | tf_op jit(solution)/shard_map/dot_general | solution.py:42
  181.4 3.3 fusion.19
  184.7 4.9 %all-to-all-start.4 = ((bf16[16,128,512]{2,1,0:T(8,128)(2,1)}), bf16[16,128,512]{2,1,0:T(8,128)(2,1)S(1)}, u32[]{:S(2)}, u32[]{:S(2)}) async-start(bf16[16,128,512]{2,1,0:T(8,128)(2,1)} %bitcast.106), calls=%async_computation.4 | async-start | bytes 4194304 | tf_op jit(solution)/shard_map/all_to_all | solution.py:55
  189.7 33.0 %reduce-scatter.2.cloned.1.call-done = bf16[1024,128]{1,0:T(8,128)(2,1)} async-done(((bf16[4096,128]{1,0:T(8,128)(2,1)}), bf16[1024,128]{1,0:T(8,128)(2,1)}) %reduce-scatter.2.cloned.1.call-update) | async-done | bytes 262160 | tf_op jit(solution)/shard_map/reduce_scatter | solution.py:146
  222.7 33.2 %all-to-all-done.4 = bf16[16,128,512]{2,1,0:T(8,128)(2,1)S(1)} async-done(((bf16[16,128,512]{2,1,0:T(8,128)(2,1)}), bf16[16,128,512]{2,1,0:T(8,128)(2,1)S(1)}, u32[]{:S(2)}, u32[]{:S(2)}) %all-to-all-start.4) | async-done | bytes 2097184 | tf_op jit(solution)/shard_map/all_to_all | solution.py:55
  255.9 4.6 %all-to-all-start.3 = ((bf16[16,128,512]{2,1,0:T(8,128)(2,1)}), bf16[16,128,512]{2,1,0:T(8,128)(2,1)}, u32[]{:S(2)}, u32[]{:S(2)}) async-start(bf16[16,128,512]{2,1,0:T(8,128)(2,1)} %bitcast.18), calls=%async_computation.3 | async-start | bytes 4194304 | tf_op jit(solution)/shard_map/all_to_all | solution.py:55
  260.5 5.7 %copy.141 = f32[2048,512]{0,1:T(8,128)} copy(f32[2048,512]{1,0:T(8,128)} %param.7) | data formatting | bytes 8388608 | tf_op args[0]
  266.3 2.1 convert_reduce_fusion.1
  268.3 2.1 convert_reduce_fusion
  270.4 7.2 %fusion.3 = f32[2048,512]{0,1:T(8,128)} fusion(bf16[2048,512]{1,0:T(8,128)(2,1)S(1)} %bitcast.105, s32[2048]{0:T(1024)S(1)} %bitcast.125), kind=kOutput, calls=%fused_computation.10 | convolution fusion | flops 4299161600 | bytes 6299648 | tf_op jit(solution)/shard_map/dot_general | solution.py:42
  277.6 64.2 %all-to-all-done.3 = bf16[16,128,512]{2,1,0:T(8,128)(2,1)} async-done(((bf16[16,128,512]{2,1,0:T(8,128)(2,1)}), bf16[16,128,512]{2,1,0:T(8,128)(2,1)}, u32[]{:S(2)}, u32[]{:S(2)}) %all-to-all-start.3) | async-done | bytes 2097184 | tf_op jit(solution)/shard_map/all_to_all | solution.py:55
  341.8 12.2 %multiply_reduce_fusion.1 = (f32[2048]{0:T(1024)S(1)}, f32[2048,512]{0,1:T(8,128)}) fusion(f32[2048,512]{0,1:T(8,128)} %copy.141, f32[2048]{0:T(1024)S(1)} %multiply_multiply_fusion, f32[2048,512]{0,1:T(8,128)} %fusion.3, bf16[2048,512]{1,0:T(8,128)(2,1)} %bitcast.21, s32[2048]{0:T(1024)S(1)} %bitcast.122), kind=kOutput, calls=%fused_computation.29 | convolution fusion | flops 4306499584 | bytes 14704640 | tf_op jit(solution)/shard_map/dot_general | solution.py:42
  353.9 3.9 multiply_reduce_fusion
  358.0 5.5 %all-reduce = (f32[2048]{0:T(1024)S(1)}, f32[4096]{0:T(1024)S(1)}) all-reduce(f32[2048]{0:T(1024)S(1)} %get-tuple-element.75, f32[4096]{0:T(1024)S(1)} %bitcast.119), channel_id=1, replica_groups=mesh['ent'=16,'dim'=2] {'dim'}, use_global_device_ids=true, to_apply=%region_11.12 | all-reduce | flops 6144 | bytes 49152 | tf_op jit(solution)/shard_map/psum | solution.py:218
  363.5 6.7 %multiply_subtract_fusion = f32[2048,512]{0,1:T(8,128)} fusion(f32[2048,512]{0,1:T(8,128)} %copy.141, f32[2048,512]{0,1:T(8,128)} %get-tuple-element.76, f32[2048]{0:T(1024)S(1)} %rsqrt_multiply_fusion.1), kind=kLoop, calls=%fused_computation.28 | loop fusion | flops 2097152 | bytes 12591104 | tf_op jit(solution)/shard_map/sub | solution.py:157
  370.2 5.3 %copy.147 = f32[2048,512]{1,0:T(8,128)} copy(f32[2048,512]{0,1:T(8,128)} %multiply_subtract_fusion) | data formatting | bytes 8388608
  375.5 5.3 %convert_element_type.247 = f32[16384,128]{1,0:T(8,128)} convert(bf16[16384,128]{1,0:T(8,128)(2,1)} %all-gather.4.cloned.1.call-done) | non-fusion elementwise | flops 2097152 | bytes 12582912 | tf_op jit(solution)/shard_map/convert_element_type | solution.py:151
  380.8 12.0 %copy.146 = f32[4,1024,4,128]{3,2,1,0:T(4,128)} copy(f32[4,1024,4,128]{3,1,2,0:T(8,128)} %bitcast.75) | data formatting | bytes 16777216 | tf_op jit(solution)/shard_map/convert_element_type | solution.py:151
  392.8 9.6 %fusion.6 = f32[4096,512]{1,0:T(8,128)} fusion(f32[4096,512]{1,0:T(8,128)} %param.10, f32[512,8,4,128]{3,2,1,0:T(4,128)} %bitcast.76, f32[4096]{0:T(1024)S(1)} %rsqrt_multiply_fusion), kind=kLoop, calls=%fused_computation.15 | loop fusion | flops 4194304 | bytes 25182208 | tf_op jit(solution)/shard_map/sub | solution.py:157
  (95 shorter events, 6.0 us)
Async XLA Ops:
  9.1 130.0 %copy-start.12 = (s32[768]{0:T(1024)}, s32[768]{0:T(1024)S(1)}, u32[]{:S(2)}) copy-start(s32[768]{0:T(1024)S(1)} %get-tuple-element.70) | copy-start | bytes 9220
  11.9 10.9 %all-to-all-start = ((s32[16,2,128]{2,1,0:T(2,128)}), s32[16,2,128]{2,1,0:T(2,128)S(1)}, u32[]{:S(2)}, u32[]{:S(2)}) async-start(s32[16,2,128]{2,1,0:T(2,128)} %pad_add_fusion), calls=%async_computation | async-start | bytes 32768 | tf_op jit(solution)/shard_map/all_to_all | solution.py:179
  32.0 54.7 %all-to-all-start.1 = ((bf16[16,128,512]{2,1,0:T(8,128)(2,1)}), bf16[16,128,512]{2,1,0:T(8,128)(2,1)}, u32[]{:S(2)}, u32[]{:S(2)}) async-start(bf16[16,128,512]{2,1,0:T(8,128)(2,1)} %bitcast.78), calls=%async_computation.1 | async-start | bytes 4194304 | tf_op jit(solution)/shard_map/all_to_all | solution.py:55
  86.7 52.5 %all-to-all-start.2 = ((bf16[16,128,512]{2,1,0:T(8,128)(2,1)}), bf16[16,128,512]{2,1,0:T(8,128)(2,1)}, u32[]{:S(2)}, u32[]{:S(2)}) async-start(bf16[16,128,512]{2,1,0:T(8,128)(2,1)} %bitcast.77), calls=%async_computation.2 | async-start | bytes 4194304 | tf_op jit(solution)/shard_map/all_to_all | solution.py:55
  95.0 0.7 copy-start.3
  101.4 0.8 copy-start
  107.5 1.4 copy-start.4
  107.5 1.7 copy-start.7
  143.6 6.5 %copy-start.1 = (bf16[256,4,2,64]{0,3,2,1:T(8,128)(2,1)}, bf16[256,4,2,64]{0,3,2,1:T(8,128)(2,1)S(1)}, u32[]{:S(2)}) copy-start(bf16[256,4,2,64]{0,3,2,1:T(8,128)(2,1)S(1)} %pad_maximum_fusion.7) | copy-start | bytes 786436
  153.9 4.5 %copy-start.5 = (f32[256,512]{0,1:T(8,128)S(1)}, f32[256,512]{0,1:T(8,128)}, u32[]{:S(2)}) copy-start(f32[256,512]{0,1:T(8,128)} %get-tuple-element.74) | copy-start | bytes 1572868
  158.5 6.5 %copy-start.2 = (bf16[256,4,2,64]{0,3,2,1:T(8,128)(2,1)S(1)}, bf16[256,4,2,64]{0,3,2,1:T(8,128)(2,1)}, u32[]{:S(2)}) copy-start(bf16[256,4,2,64]{0,3,2,1:T(8,128)(2,1)} %copy-done.1) | copy-start | bytes 786436
  158.5 12.7 %copy-start.10 = (s32[1,2048]{1,0:T(1,128)S(1)}, s32[1,2048]{1,0:T(1,128)}, u32[]{:S(2)}) copy-start(s32[1,2048]{1,0:T(1,128)} %all-gather) | copy-start | bytes 24580
  160.8 10.3 %all-to-all-start.5 = ((bf16[4,512,128]{2,1,0:T(8,128)(2,1)}), bf16[4,512,128]{2,1,0:T(8,128)(2,1)S(1)}, u32[]{:S(2)}, u32[]{:S(2)}) async-start(bf16[4,512,128]{2,1,0:T(8,128)(2,1)} %maximum_bitcast_fusion), calls=%async_computation.5 | async-start | bytes 1048576 | tf_op jit(solution)/shard_map/all_to_all | solution.py:137
  164.3 58.4 %reduce-scatter.2.cloned.1.call-start = ((), (), s32[]{:S(2)}) async-start(), calls=%async_computation.7 | async-start | bytes 1310720 | tf_op jit(solution)/shard_map/reduce_scatter | solution.py:146
  171.1 10.2 %copy-start.6 = (bf16[256,512]{1,0:T(8,128)(2,1)S(1)}, bf16[256,512]{1,0:T(8,128)(2,1)}, u32[]{:S(2)}) copy-start(bf16[256,512]{1,0:T(8,128)(2,1)} %copy.138) | copy-start | bytes 786436
  171.1 10.2 %copy-start.13 = (s32[768]{0:T(1024)S(1)}, s32[768]{0:T(1024)}, u32[]{:S(2)}) copy-start(s32[768]{0:T(1024)} %copy-done.12) | copy-start | bytes 9220
  184.7 71.2 %all-to-all-start.4 = ((bf16[16,128,512]{2,1,0:T(8,128)(2,1)}), bf16[16,128,512]{2,1,0:T(8,128)(2,1)S(1)}, u32[]{:S(2)}, u32[]{:S(2)}) async-start(bf16[16,128,512]{2,1,0:T(8,128)(2,1)} %bitcast.106), calls=%async_computation.4 | async-start | bytes 4194304 | tf_op jit(solution)/shard_map/all_to_all | solution.py:55
  189.6 164.3 %all-gather.4.cloned.1.call-start = ((), (), s32[]{:S(2)}) async-start(), calls=%async_computation.8 | async-start | bytes 4456448 | tf_op jit(solution)/shard_map/all_gather | solution.py:149
  255.9 85.8 %all-to-all-start.3 = ((bf16[16,128,512]{2,1,0:T(8,128)(2,1)}), bf16[16,128,512]{2,1,0:T(8,128)(2,1)}, u32[]{:S(2)}, u32[]{:S(2)}) async-start(bf16[16,128,512]{2,1,0:T(8,128)(2,1)} %bitcast.18), calls=%async_computation.3 | async-start | bytes 4194304 | tf_op jit(solution)/shard_map/all_to_all | solution.py:55
  260.5 9.9 %copy-start.11 = (s32[2048]{0:T(1024)S(1)}, s32[2048]{0:T(1024)}, u32[]{:S(2)}) copy-start(s32[2048]{0:T(1024)} %param.9) | copy-start | bytes 24580
  353.9 9.5 %copy-start.9 = (f32[2048]{0:T(1024)S(1)}, f32[2048]{0:T(1024)}, u32[]{:S(2)}) copy-start(f32[2048]{0:T(1024)} %param.8) | copy-start | bytes 24580
  380.8 12.0 %copy-start.8 = (f32[4096]{0:T(1024)S(1)}, f32[4096]{0:T(1024)}, u32[]{:S(2)}) copy-start(f32[4096]{0:T(1024)} %param.11) | copy-start | bytes 49156
Sparse Core Ops, SparseCore 0:
  181.5 41.1 reduce-scatter.1
  225.5 113.7 all-gather.3
